TPU v7x, 32 devices: a whole 2x2x4 slice. The times are simulated.
32 devices in a mesh: tok: 8 (over y, x, core), blk: 4 (over z).
Axes of the slice: x: 2, y: 2, z: 4, core: 2. Of those that a mesh axis runs over, the one named last changes fastest.
Arguments:
- activations: bfloat16 [4096, 4096], P('tok', 'blk'), may hold values from -52 to 52, as said below
- out_grads: bfloat16 [4096, 4096], P('tok', 'blk'), may hold values from -52 to 52, as said below
Outputs:
- act_inverse: float32 [4096, 4096], P(('tok', 'blk'))
- grad_inverse: float32 [4096, 4096], P(('tok', 'blk'))
Inputs may be any that keep to these rules, and one draw needn't show every extreme that they name: `activations`: real entries. `out_grads`: real entries.
All inputs are finite; a program needn't handle non-finite values.
Results may differ from a plain program's by a relative error of at most 0.02.
Values may be sent and summed in bfloat16 or wider, within the bound.
A program may use at most 64 MiB of HBM per device.

v0:
```python
import jax
import jax.numpy as jnp
from jax import lax
from jax.sharding import PartitionSpec as P

D = 4096
damping = 0.3
epsilon = 1e-06
divisor = 2.0


def column_squares(data):
    values = data.astype(jnp.float32)
    return jnp.sum(values * values, axis=0)


def fold_product(row_block, tile):
    return jnp.dot(
        row_block,
        lax.all_gather(tile, "tok", axis=0, tiled=True),
        preferred_element_type=jnp.float32,
    )


def newton_steps(scaled, identity):
    half = scaled.astype(jnp.bfloat16)
    row_block = lax.all_gather(half, "blk", axis=1, tiled=True)
    square = fold_product(row_block, half)
    cube = fold_product(row_block, square.astype(jnp.bfloat16))
    return 4.0 * identity - 6.0 * scaled + 4.0 * square - cube


def body(activations, out_grads):
    tok_count = lax.axis_size("tok")
    blk_count = lax.axis_size("blk")
    tok_id = lax.axis_index("tok")
    blk_id = lax.axis_index("blk")
    token_count = activations.shape[0] * tok_count
    tile_rows = D // tok_count
    tile_cols = D // blk_count
    full_acts, full_grads = (
        lax.all_gather(activations, "blk", axis=1, tiled=True),
        lax.all_gather(out_grads, "blk", axis=1, tiled=True),
    )
    sums_act, sums_grad = (
        lax.psum(column_squares(full_acts).astype(jnp.bfloat16), "tok").astype(jnp.float32),
        lax.psum(column_squares(full_grads).astype(jnp.bfloat16), "tok").astype(jnp.float32),
    )
    row_ids = tok_id * tile_rows + jnp.arange(tile_rows, dtype=jnp.int32)
    col_ids = blk_id * tile_cols + jnp.arange(tile_cols, dtype=jnp.int32)
    identity = (row_ids[:, None] == col_ids[None, :]).astype(jnp.float32)

    def damped_tile(full, local, sums):
        gram_tile = lax.psum_scatter(
            lax.dot_general(
                full, local, (((0,), (0,)), ((), ())), preferred_element_type=jnp.float32
            ).astype(jnp.bfloat16),
            "tok",
            scatter_dimension=0,
            tiled=True,
        ).astype(jnp.float32)
        inverse = lax.rsqrt(sums / token_count + epsilon)
        inverse_rows = lax.dynamic_slice_in_dim(inverse, tok_id * tile_rows, tile_rows)
        inverse_cols = lax.dynamic_slice_in_dim(inverse, blk_id * tile_cols, tile_cols)
        return (
            gram_tile / token_count * inverse_rows[:, None] * inverse_cols[None, :]
            + damping * identity
        )

    damped_act = damped_tile(full_acts, activations, sums_act)
    damped_grad = damped_tile(full_grads, out_grads, sums_grad)
    results = []
    for damped in (damped_act, damped_grad):
        scaled = damped / divisor
        result_tile = newton_steps(scaled, identity)
        results.append(
            lax.all_to_all(
                result_tile.astype(jnp.bfloat16), "blk", split_axis=0, concat_axis=1, tiled=True
            ).astype(result_tile.dtype)
        )
    return (results[0], results[1])


def solution(mesh):
    placed = (P("tok", "blk"), P("tok", "blk"))
    return jax.shard_map(
        body,
        mesh=mesh,
        in_specs=placed,
        out_specs=(P(("tok", "blk"), None), P(("tok", "blk"), None)),
        check_vma=False,
    )
```

profile of v0, /device:TPU:0, one launch (start us, length us, event | category | flops | bytes accessed | tf_op | source)
XLA Modules:
  0.0 763.5 jit_solution(1316433522095304969)
XLA Ops:
  7.2 0.0 all-gather.9.cloned.1.call-start
  7.2 0.7 all-gather.9.cloned.1.call-update
  7.9 0.0 all-gather.17.cloned.1.call-start
  8.0 0.7 all-gather.17.cloned.1.call-update
  8.7 0.0 reduce-scatter.3.cloned.1.call-start
  8.7 84.3 %all-gather.9.cloned.1.call-done = bf16[512,4096]{1,0:T(8,128)(2,1)} async-done(((bf16[512,1024]{1,0:T(8,128)(2,1)}), bf16[512,4096]{1,0:T(8,128)(2,1)}) %all-gather.9.cloned.1.call-update) | async-done | bytes 4194320 | tf_op jit(solution)/shard_map/all_gather | solution.py:42
  93.0 9.1 %convolution_convert_fusion.1 = bf16[4096,1024]{1,0:T(8,128)(2,1)} fusion(bf16[512,4096]{1,0:T(8,128)(2,1)} %all-gather.9.cloned.1.call-done, bf16[512,1024]{1,0:T(8,128)(2,1)S(1)} %copy-done.1), kind=kOutput, calls=%fused_computation.3 | convolution fusion | flops 4299161600 | bytes 13631488 | tf_op jit(solution)/shard_map/dot_general | solution.py:55
  102.1 0.0 reduce-scatter.3.cloned.1.call-update
  102.2 0.0 reduce-scatter.5.cloned.1.call-start
  102.2 71.7 %all-gather.17.cloned.1.call-done = bf16[512,4096]{1,0:T(8,128)(2,1)} async-done(((bf16[512,1024]{1,0:T(8,128)(2,1)}), bf16[512,4096]{1,0:T(8,128)(2,1)}) %all-gather.17.cloned.1.call-update) | async-done | bytes 4194320 | tf_op jit(solution)/shard_map/all_gather | solution.py:43
  173.9 9.0 %convolution_convert_fusion = bf16[4096,1024]{1,0:T(8,128)(2,1)} fusion(bf16[512,4096]{1,0:T(8,128)(2,1)} %all-gather.17.cloned.1.call-done, bf16[512,1024]{1,0:T(8,128)(2,1)S(1)} %copy-done.2), kind=kOutput, calls=%fused_computation.2 | convolution fusion | flops 4299161600 | bytes 13631488 | tf_op jit(solution)/shard_map/dot_general | solution.py:55
  182.9 0.0 reduce-scatter.5.cloned.1.call-update
  182.9 0.0 all-gather.19.cloned.1.call-start
  183.0 4.2 multiply_reduce_fusion
  187.1 1.0 copy-done
  188.2 0.9 multiply_reduce_fusion.1
  189.1 24.5 %all-reduce = (bf16[4096]{0:T(1024)(128)(2,1)S(1)}, bf16[4096]{0:T(1024)(128)(2,1)S(1)}) all-reduce(bf16[4096]{0:T(1024)(128)(2,1)S(1)} %multiply_reduce_fusion.1, bf16[4096]{0:T(1024)(128)(2,1)S(1)} %multiply_reduce_fusion), channel_id=1, replica_groups=mesh['tok'=8,'blk'=4] {'tok'}, use_global_device_ids=true, to_apply=%region_2.0 | all-reduce | flops 8192 | bytes 32768 | tf_op jit(solution)/shard_map/psum | solution.py:46
  213.6 0.1 dynamic-slice_multiply_fusion
  213.7 0.1 dynamic-slice_multiply_fusion.1
  213.8 33.8 %reduce-scatter.3.cloned.1.call-done = bf16[512,1024]{1,0:T(8,128)(2,1)} async-done(((bf16[4096,1024]{1,0:T(8,128)(2,1)}), bf16[512,1024]{1,0:T(8,128)(2,1)}) %reduce-scatter.3.cloned.1.call-update) | async-done | bytes 1048592 | tf_op jit(solution)/shard_map/reduce_scatter | solution.py:54
  247.6 74.8 %reduce-scatter.5.cloned.1.call-done = bf16[512,1024]{1,0:T(8,128)(2,1)} async-done(((bf16[4096,1024]{1,0:T(8,128)(2,1)}), bf16[512,1024]{1,0:T(8,128)(2,1)}) %reduce-scatter.5.cloned.1.call-update) | async-done | bytes 1048592 | tf_op jit(solution)/shard_map/reduce_scatter | solution.py:54
  322.4 3.8 multiply_convert_fusion
  326.2 0.0 all-gather.21.cloned.1.call-start
  326.3 0.5 all-gather.21.cloned.1.call-update
  326.8 0.0 all-gather.11.cloned.1.call-start
  326.9 0.7 all-gather.11.cloned.1.call-update
  327.6 0.0 all-gather.13.cloned.1.call-start
  327.6 0.7 all-gather.13.cloned.1.call-update
  328.3 0.0 all-gather.23.cloned.1.call-start
  328.4 78.8 %all-gather.19.cloned.1.call-done = bf16[512,4096]{1,0:T(8,128)(2,1)} async-done(((bf16[512,1024]{1,0:T(8,128)(2,1)}), bf16[512,4096]{1,0:T(8,128)(2,1)}) %all-gather.19.cloned.1.call-update) | async-done | bytes 4194320 | tf_op jit(solution)/shard_map/all_gather | solution.py:27
  407.1 55.1 %all-gather.21.cloned.1.call-done = bf16[4096,1024]{1,0:T(8,128)(2,1)} async-done(((bf16[512,1024]{1,0:T(8,128)(2,1)}), bf16[4096,1024]{1,0:T(8,128)(2,1)}) %all-gather.21.cloned.1.call-update) | async-done | bytes 8388624 | tf_op jit(solution)/shard_map/all_gather | solution.py:20
  462.2 10.1 %fusion.9 = (bf16[512,1024]{1,0:T(8,128)(2,1)}, f32[512,1024]{1,0:T(8,128)S(1)}) fusion(bf16[512,4096]{1,0:T(8,128)(2,1)} %all-gather.19.cloned.1.call-done, bf16[4096,1024]{1,0:T(8,128)(2,1)} %all-gather.21.cloned.1.call-done), kind=kOutput, calls=%fused_computation.26 | convolution fusion | flops 4295491584 | bytes 15728640 | tf_op jit(solution)/shard_map/dot_general | solution.py:18
  472.4 0.0 all-gather.23.cloned.1.call-update
  472.4 0.2 all-gather.15.cloned.1.call-start
  472.6 72.5 %all-gather.11.cloned.1.call-done = bf16[512,4096]{1,0:T(8,128)(2,1)} async-done(((bf16[512,1024]{1,0:T(8,128)(2,1)}), bf16[512,4096]{1,0:T(8,128)(2,1)}) %all-gather.11.cloned.1.call-update) | async-done | bytes 4194320 | tf_op jit(solution)/shard_map/all_gather | solution.py:27
  545.1 55.2 %all-gather.13.cloned.1.call-done = bf16[4096,1024]{1,0:T(8,128)(2,1)} async-done(((bf16[512,1024]{1,0:T(8,128)(2,1)}), bf16[4096,1024]{1,0:T(8,128)(2,1)}) %all-gather.13.cloned.1.call-update) | async-done | bytes 8388624 | tf_op jit(solution)/shard_map/all_gather | solution.py:20
  600.4 10.8 %fusion.8 = (bf16[512,1024]{1,0:T(8,128)(2,1)}, f32[512,1024]{1,0:T(8,128)}) fusion(bf16[512,4096]{1,0:T(8,128)(2,1)} %all-gather.11.cloned.1.call-done, bf16[4096,1024]{1,0:T(8,128)(2,1)} %all-gather.13.cloned.1.call-done), kind=kOutput, calls=%fused_computation.25 | convolution fusion | flops 4295491584 | bytes 15728640 | tf_op jit(solution)/shard_map/dot_general | solution.py:18
  611.2 45.4 %all-gather.23.cloned.1.call-done = bf16[4096,1024]{1,0:T(8,128)(2,1)} async-done(((bf16[512,1024]{1,0:T(8,128)(2,1)}), bf16[4096,1024]{1,0:T(8,128)(2,1)}) %all-gather.23.cloned.1.call-update) | async-done | bytes 8388624 | tf_op jit(solution)/shard_map/all_gather | solution.py:20
  656.6 10.6 %fusion.7 = bf16[512,1024]{1,0:T(8,128)(2,1)} fusion(f32[512,1024]{1,0:T(8,128)S(1)} %get-tuple-element.9, bf16[512,1024]{1,0:T(8,128)(2,1)S(1)} %copy-done.4, bf16[512,4096]{1,0:T(8,128)(2,1)} %all-gather.19.cloned.1.call-done, bf16[4096,1024]{1,0:T(8,128)(2,1)} %all-gather.23.cloned.1.call-done, f32[1024]{0:T(1024)S(1)} %dynamic_slice.15, ...), kind=kOutput, calls=%fused_computation.14 | convolution fusion | flops 4301783040 | bytes 16789504 | tf_op jit(solution)/shard_map/dot_general | solution.py:18
  667.2 4.7 all-to-all-start.1
  671.9 41.2 %all-gather.15.cloned.1.call-done = bf16[4096,1024]{1,0:T(8,128)(2,1)} async-done(((bf16[512,1024]{1,0:T(8,128)(2,1)}), bf16[4096,1024]{1,0:T(8,128)(2,1)}) %all-gather.15.cloned.1.call-update) | async-done | bytes 8388624 | tf_op jit(solution)/shard_map/all_gather | solution.py:20
  713.2 11.1 %fusion.4 = bf16[512,1024]{1,0:T(8,128)(2,1)} fusion(f32[512,1024]{1,0:T(8,128)} %get-tuple-element.7, bf16[512,1024]{1,0:T(8,128)(2,1)S(1)} %copy-done.3, bf16[512,4096]{1,0:T(8,128)(2,1)} %all-gather.11.cloned.1.call-done, bf16[4096,1024]{1,0:T(8,128)(2,1)} %all-gather.15.cloned.1.call-done, f32[1024]{0:T(1024)S(1)} %dynamic_slice.13, ...), kind=kOutput, calls=%fused_computation.11 | convolution fusion | flops 4301783040 | bytes 16789504 | tf_op jit(solution)/shard_map/dot_general | solution.py:18
  724.3 4.6 all-to-all-start
  728.9 0.2 convert_bitcast_fusion
  729.1 1.5 copy.7
  730.6 24.4 %all-to-all-done = bf16[4,128,1024]{2,1,0:T(8,128)(2,1)S(1)} async-done(((bf16[4,128,1024]{2,1,0:T(8,128)(2,1)}), bf16[4,128,1024]{2,1,0:T(8,128)(2,1)S(1)}, u32[]{:S(2)}, u32[]{:S(2)}) %all-to-all-start) | async-done | bytes 1048608 | tf_op jit(solution)/shard_map/all_to_all | solution.py:77
  755.0 0.2 convert_bitcast_fusion.1
  755.2 1.5 copy.6
  (17 shorter events, 0.1 us)
Async XLA Ops:
  7.2 85.9 %copy-start.1 = (bf16[512,1024]{1,0:T(8,128)(2,1)S(1)}, bf16[512,1024]{1,0:T(8,128)(2,1)}, u32[]{:S(2)}) copy-start(bf16[512,1024]{1,0:T(8,128)(2,1)} %param.2) | copy-start | bytes 3145732
  7.2 85.9 %all-gather.9.cloned.1.call-start = ((), (), s32[]{:S(2)}) async-start(), calls=%async_computation.4 | async-start | bytes 5242880 | tf_op jit(solution)/shard_map/all_gather | solution.py:42
  7.9 166.0 %all-gather.17.cloned.1.call-start = ((), (), s32[]{:S(2)}) async-start(), calls=%async_computation.9 | async-start | bytes 5242880 | tf_op jit(solution)/shard_map/all_gather | solution.py:43
  8.7 238.9 %reduce-scatter.3.cloned.1.call-start = ((), (), s32[]{:S(2)}) async-start(), calls=%async_computation.5 | async-start | bytes 9437184 | tf_op jit(solution)/shard_map/reduce_scatter | solution.py:54
  102.1 71.7 %copy-start.2 = (bf16[512,1024]{1,0:T(8,128)(2,1)S(1)}, bf16[512,1024]{1,0:T(8,128)(2,1)}, u32[]{:S(2)}) copy-start(bf16[512,1024]{1,0:T(8,128)(2,1)} %param.3) | copy-start | bytes 3145732
  102.2 220.2 %reduce-scatter.5.cloned.1.call-start = ((), (), s32[]{:S(2)}) async-start(), calls=%async_computation.10 | async-start | bytes 9437184 | tf_op jit(solution)/shard_map/reduce_scatter | solution.py:54
  182.9 224.3 %all-gather.19.cloned.1.call-start = ((), (), s32[]{:S(2)}) async-start(), calls=%async_computation.11 | async-start | bytes 5242880 | tf_op jit(solution)/shard_map/all_gather | solution.py:27
  183.0 5.2 copy-start
  326.2 136.0 %all-gather.21.cloned.1.call-start = ((), (), s32[]{:S(2)}) async-start(), calls=%async_computation.12 | async-start | bytes 9437184 | tf_op jit(solution)/shard_map/all_gather | solution.py:20
  326.8 218.3 %all-gather.11.cloned.1.call-start = ((), (), s32[]{:S(2)}) async-start(), calls=%async_computation.6 | async-start | bytes 5242880 | tf_op jit(solution)/shard_map/all_gather | solution.py:27
  327.6 272.8 %all-gather.13.cloned.1.call-start = ((), (), s32[]{:S(2)}) async-start(), calls=%async_computation.7 | async-start | bytes 9437184 | tf_op jit(solution)/shard_map/all_gather | solution.py:20
  328.3 328.3 %all-gather.23.cloned.1.call-start = ((), (), s32[]{:S(2)}) async-start(), calls=%async_computation.13 | async-start | bytes 9437184 | tf_op jit(solution)/shard_map/all_gather | solution.py:20
  472.4 184.2 %copy-start.4 = (bf16[512,1024]{1,0:T(8,128)(2,1)S(1)}, bf16[512,1024]{1,0:T(8,128)(2,1)}, u32[]{:S(2)}) copy-start(bf16[512,1024]{1,0:T(8,128)(2,1)} %reduce-scatter.5.cloned.1.call-done) | copy-start | bytes 3145732
  472.4 240.8 %all-gather.15.cloned.1.call-start = ((), (), s32[]{:S(2)}) async-start(), calls=%async_computation.8 | async-start | bytes 9437184 | tf_op jit(solution)/shard_map/all_gather | solution.py:20
  667.2 46.0 %copy-start.3 = (bf16[512,1024]{1,0:T(8,128)(2,1)S(1)}, bf16[512,1024]{1,0:T(8,128)(2,1)}, u32[]{:S(2)}) copy-start(bf16[512,1024]{1,0:T(8,128)(2,1)} %reduce-scatter.3.cloned.1.call-done) | copy-start | bytes 3145732
  667.2 57.0 %all-to-all-start.1 = ((bf16[4,128,1024]{2,1,0:T(8,128)(2,1)}), bf16[4,128,1024]{2,1,0:T(8,128)(2,1)S(1)}, u32[]{:S(2)}, u32[]{:S(2)}) async-start(bf16[4,128,1024]{2,1,0:T(8,128)(2,1)} %bitcast.2), calls=%async_computation.3 | async-start | bytes 2097152 | tf_op jit(solution)/shard_map/all_to_all | solution.py:77
  724.3 30.7 %all-to-all-start = ((bf16[4,128,1024]{2,1,0:T(8,128)(2,1)}), bf16[4,128,1024]{2,1,0:T(8,128)(2,1)S(1)}, u32[]{:S(2)}, u32[]{:S(2)}) async-start(bf16[4,128,1024]{2,1,0:T(8,128)(2,1)} %bitcast), calls=%async_computation.1 | async-start | bytes 2097152 | tf_op jit(solution)/shard_map/all_to_all | solution.py:77
Sparse Core Ops, SparseCore 0:
  9.6 83.4 all-gather.8
  94.6 79.2 all-gather.16
  177.3 70.1 reduce-scatter.2
  250.9 71.4 reduce-scatter.4
  326.4 80.7 all-gather.18
  409.5 52.7 all-gather.20
  464.4 80.7 all-gather.10
  547.6 52.7 all-gather.12
  602.3 54.2 all-gather.22
  658.9 54.2 all-gather.14
where the time goes:
time: 764 us
  waiting for transfers between devices  641 us (84%)
  matrix products  60.7 us (8%)
  blocking collectives  24.5 us (3%)
  between operations  14.3 us (2%)
  starting transfers between devices  9.9 us (1%)
  other arithmetic  9.53 us (1%)
    all_gather x4, waiting for transfers between devices, fold_product(): lax.all_gather(tile, 'tok', axis=0, tiled=True)  197 us
    all_gather x2, waiting for transfers between devices, newton_steps(): row_block = lax.all_gather(half, 'blk', axis=1, tiled=True)  151 us
    reduce_scatter x2, waiting for transfers between devices, damped_tile(): lax.psum_scatter(lax.dot_general(full, local, (((0,), (0,)), ((), ())), p...  109 us
    all_gather x1, waiting for transfers between devices, body(): lax.all_gather(activations, 'blk', axis=1, tiled=True)  84.3 us
    all_gather x1, waiting for transfers between devices, body(): lax.all_gather(out_grads, 'blk', axis=1, tiled=True)  71.7 us
    dot_general x4, matrix products, fold_product(): jnp.dot(row_block, lax.all_gather(tile, 'tok', axis=0, tiled=True), prefe...  42.6 us
    psum x1, blocking collectives, body(): lax.psum(column_squares(full_acts).astype(jnp.bfloat16), 'tok')  24.5 us
    all_to_all x2, waiting for transfers between devices, body(): lax.all_to_all(result_tile.astype(jnp.bfloat16), 'blk', split_axis=0, con...  24.4 us
  transfers between devices with their start and end apart: 12, of which 11 were waited for; matrix products, arithmetic and copies ran while one was open for 9% of the time, Pallas kernels for 0%

commit v1 on v0

--- a/solution.py
+++ b/solution.py
@@ -1,3 +1,4 @@
+import functools
 import jax
 import jax.numpy as jnp
 from jax import lax
@@ -7,6 +8,25 @@
 damping = 0.3
 epsilon = 1e-06
 divisor = 2.0
+
+
+def bind_group(x_in, which_axis):
+    total_devices = lax.axis_size(which_axis)
+    nodes = []
+    for j0 in tuple(range(1, total_devices)):
+        nodes.append((j0 - 1, j0))
+    raw_out = nodes + [(total_devices - 1, 0)]
+    found_now = x_in
+    found = [found_now]
+    for _ in tuple(range(total_devices - 1)):
+        found_now = lax.ppermute(found_now, which_axis, raw_out)
+        found += [found_now]
+    u1 = jnp.concatenate([*reversed(found)], 1)
+    n_now = jnp.roll(u1, (lax.axis_index(which_axis) + 1) * found_now.shape[1], 1)
+    return n_now
+
+
+obtain_screen = functools.partial(bind_group, which_axis="blk")
 
 
 def column_squares(data):
@@ -24,7 +44,7 @@
 
 def newton_steps(scaled, identity):
     half = scaled.astype(jnp.bfloat16)
-    row_block = lax.all_gather(half, "blk", axis=1, tiled=True)
+    row_block = obtain_screen(half)
     square = fold_product(row_block, half)
     cube = fold_product(row_block, square.astype(jnp.bfloat16))
     return 4.0 * identity - 6.0 * scaled + 4.0 * square - cube

time: 764 us -> 619 us (0.81)
  waiting for transfers between devices: 641 us -> 475 us
  other arithmetic: 9.53 us -> 26.8 us
    all_gather x4, waiting for transfers between devices: 197 us -> 36.3 us  [fold_product(): lax.all_gather(tile, 'tok', axis=0, tiled=True)]
    all_gather x2 -> x0, waiting for transfers between devices: 151 us -> none  [newton_steps(): row_block = lax.all_gather(half, 'blk', axis=1, tiled=True)]
    ppermute x0 -> x6, waiting for transfers between devices: none -> 149 us  [bind_group(): found_now = lax.ppermute(found_now, which_axis, raw_out)]
    concatenate x0 -> x2, other arithmetic: none -> 17.2 us  [bind_group(): jnp.roll(u1, (lax.axis_index(which_axis) + 1) * found_now.shape[1], 1)]
    all_gather x1, waiting for transfers between devices: 84.3 us -> 70.2 us  [body(): lax.all_gather(activations, 'blk', axis=1, tiled=True)]
    all_gather x1, waiting for transfers between devices: 71.7 us -> 84.3 us  [body(): lax.all_gather(out_grads, 'blk', axis=1, tiled=True)]
  transfers between devices with their start and end apart: 12 -> 16, of which waited for: 11 -> 12; matrix products, arithmetic and copies ran while one was open for 9% -> 14% of each run, Pallas kernels for 0% -> 0%
where the time goes in v1:
time: 619 us
  waiting for transfers between devices  475 us (77%)
  matrix products  64.1 us (10%)
  other arithmetic  26.8 us (4%)
  blocking collectives  24.5 us (4%)
  between operations  14.3 us (2%)
  starting transfers between devices  10.3 us (2%)
    ppermute x6, waiting for transfers between devices, bind_group(): found_now = lax.ppermute(found_now, which_axis, raw_out)  149 us
    reduce_scatter x2, waiting for transfers between devices, damped_tile(): lax.psum_scatter(lax.dot_general(full, local, (((0,), (0,)), ((), ())), p...  109 us
    all_gather x1, waiting for transfers between devices, body(): lax.all_gather(out_grads, 'blk', axis=1, tiled=True)  84.3 us
    all_gather x1, waiting for transfers between devices, body(): lax.all_gather(activations, 'blk', axis=1, tiled=True)  70.2 us
    dot_general x4, matrix products, fold_product(): jnp.dot(row_block, lax.all_gather(tile, 'tok', axis=0, tiled=True), prefe...  44.6 us
    all_gather x4, waiting for transfers between devices, fold_product(): lax.all_gather(tile, 'tok', axis=0, tiled=True)  36.3 us
    psum x1, blocking collectives, body(): lax.psum(column_squares(full_acts).astype(jnp.bfloat16), 'tok')  24.5 us
    all_to_all x2, waiting for transfers between devices, body(): lax.all_to_all(result_tile.astype(jnp.bfloat16), 'blk', split_axis=0, con...  24.4 us
  transfers between devices with their start and end apart: 16, of which 12 were waited for; matrix products, arithmetic and copies ran while one was open for 14% of the time, Pallas kernels for 0%

profile of v1, /device:TPU:0, one launch (start us, length us, event | category | flops | bytes accessed | tf_op | source)
XLA Modules:
  0.0 618.8 jit_solution(11465068782064229488)
XLA Ops:
  7.2 0.0 all-gather.13.cloned.1.call-start
  7.2 0.7 all-gather.13.cloned.1.call-update
  7.9 0.0 all-gather.7.cloned.1.call-start
  7.9 0.7 all-gather.7.cloned.1.call-update
  8.6 0.0 reduce-scatter.5.cloned.1.call-start
  8.7 84.3 %all-gather.13.cloned.1.call-done = bf16[512,4096]{1,0:T(8,128)(2,1)} async-done(((bf16[512,1024]{1,0:T(8,128)(2,1)}), bf16[512,4096]{1,0:T(8,128)(2,1)}) %all-gather.13.cloned.1.call-update) | async-done | bytes 4194320 | tf_op jit(solution)/shard_map/all_gather | solution.py:63
  93.0 10.5 %convolution_convert_fusion = bf16[4096,1024]{1,0:T(8,128)(2,1)} fusion(bf16[512,4096]{1,0:T(8,128)(2,1)} %all-gather.13.cloned.1.call-done, bf16[512,1024]{1,0:T(8,128)(2,1)} %param.5), kind=kOutput, calls=%fused_computation.18 | convolution fusion | flops 4299161600 | bytes 13631488 | tf_op jit(solution)/shard_map/dot_general | solution.py:75
  103.6 0.0 reduce-scatter.5.cloned.1.call-update
  103.6 0.0 reduce-scatter.3.cloned.1.call-start
  103.6 70.2 %all-gather.7.cloned.1.call-done = bf16[512,4096]{1,0:T(8,128)(2,1)} async-done(((bf16[512,1024]{1,0:T(8,128)(2,1)}), bf16[512,4096]{1,0:T(8,128)(2,1)}) %all-gather.7.cloned.1.call-update) | async-done | bytes 4194320 | tf_op jit(solution)/shard_map/all_gather | solution.py:62
  173.9 9.0 %convolution_convert_fusion.1 = bf16[4096,1024]{1,0:T(8,128)(2,1)} fusion(bf16[512,4096]{1,0:T(8,128)(2,1)} %all-gather.7.cloned.1.call-done, bf16[512,1024]{1,0:T(8,128)(2,1)S(1)} %copy-done.2), kind=kOutput, calls=%fused_computation.19 | convolution fusion | flops 4299161600 | bytes 13631488 | tf_op jit(solution)/shard_map/dot_general | solution.py:75
  182.9 0.0 all-gather.9.cloned.1.call-start
  183.0 4.2 multiply_reduce_fusion.1
  187.1 1.0 copy-done.1
  188.1 0.9 multiply_reduce_fusion
  189.0 24.5 %all-reduce = (bf16[4096]{0:T(1024)(128)(2,1)S(1)}, bf16[4096]{0:T(1024)(128)(2,1)S(1)}) all-reduce(bf16[4096]{0:T(1024)(128)(2,1)S(1)} %multiply_reduce_fusion.1, bf16[4096]{0:T(1024)(128)(2,1)S(1)} %multiply_reduce_fusion), channel_id=1, replica_groups=mesh['tok'=8,'blk'=4] {'tok'}, use_global_device_ids=true, to_apply=%region_2.0 | all-reduce | flops 8192 | bytes 32768 | tf_op jit(solution)/shard_map/psum | solution.py:66
  213.6 0.1 dynamic-slice_multiply_fusion
  213.7 0.1 dynamic-slice_multiply_fusion.1
  213.7 33.8 %reduce-scatter.5.cloned.1.call-done = bf16[512,1024]{1,0:T(8,128)(2,1)} async-done(((bf16[4096,1024]{1,0:T(8,128)(2,1)}), bf16[512,1024]{1,0:T(8,128)(2,1)}) %reduce-scatter.5.cloned.1.call-update) | async-done | bytes 1048592 | tf_op jit(solution)/shard_map/reduce_scatter | solution.py:74
  247.5 74.8 %reduce-scatter.3.cloned.1.call-done = bf16[512,1024]{1,0:T(8,128)(2,1)} async-done(((bf16[4096,1024]{1,0:T(8,128)(2,1)}), bf16[512,1024]{1,0:T(8,128)(2,1)}) %reduce-scatter.3.cloned.1.call-update) | async-done | bytes 1048592 | tf_op jit(solution)/shard_map/reduce_scatter | solution.py:74
  322.4 3.8 multiply_convert_fusion
  326.2 0.0 all-gather.15.cloned.1.call-start
  326.3 0.5 all-gather.15.cloned.1.call-update
  326.8 0.0 all-gather.11.cloned.1.call-start
  326.8 1.5 collective-permute-start
  328.4 25.3 %collective-permute-done = bf16[512,1024]{1,0:T(8,128)(2,1)S(1)} collective-permute-done((bf16[512,1024]{1,0:T(8,128)(2,1)}, bf16[512,1024]{1,0:T(8,128)(2,1)S(1)}, u32[]{:S(2)}, u32[]{:S(2)}) %collective-permute-start) | collective-permute-done | bytes 1048608 | tf_op jit(solution)/shard_map/ppermute | solution.py:22
  353.6 25.7 %collective-permute-done.1 = bf16[512,1024]{1,0:T(8,128)(2,1)S(1)} collective-permute-done((bf16[512,1024]{1,0:T(8,128)(2,1)S(1)}, bf16[512,1024]{1,0:T(8,128)(2,1)S(1)}, u32[]{:S(2)}, u32[]{:S(2)}) %collective-permute-start.1) | collective-permute-done | bytes 1048608 | tf_op jit(solution)/shard_map/ppermute | solution.py:22
  379.3 24.8 %collective-permute-done.2 = bf16[512,1024]{1,0:T(8,128)(2,1)S(1)} collective-permute-done((bf16[512,1024]{1,0:T(8,128)(2,1)S(1)}, bf16[512,1024]{1,0:T(8,128)(2,1)S(1)}, u32[]{:S(2)}, u32[]{:S(2)}) %collective-permute-start.2) | collective-permute-done | bytes 1048608 | tf_op jit(solution)/shard_map/ppermute | solution.py:22
  404.1 9.0 %fusion.10 = bf16[512,4096]{1,0:T(8,128)(2,1)} fusion(s32[]{:T(128)S(6)} %select_n.23, bf16[512,1024]{1,0:T(8,128)(2,1)S(1)} %collective-permute-done.2, bf16[512,1024]{1,0:T(8,128)(2,1)S(1)} %collective-permute-done.1, bf16[512,1024]{1,0:T(8,128)(2,1)S(1)} %collective-permute-done, bf16[512,1024]{1,0:T(8,128)(2,1)} %get-tuple-element.6), kind=kLoop, calls=%fused_computation.30 | loop fusion | flops 33554432 | bytes 8388612 | tf_op jit(solution)/shard_map/jit(_roll_dynamic)/concatenate | solution.py:25
  413.1 10.9 %fusion.22 = (bf16[512,1024]{1,0:T(8,128)(2,1)}, f32[512,1024]{1,0:T(8,128)}) fusion(bf16[512,4096]{1,0:T(8,128)(2,1)} %fusion.10, bf16[4096,1024]{1,0:T(8,128)(2,1)} %all-gather.9.cloned.1.call-done), kind=kOutput, calls=%fused_computation.55 | convolution fusion | flops 4295491584 | bytes 15728640 | tf_op jit(solution)/shard_map/dot_general | solution.py:38
  424.1 0.0 all-gather.17.cloned.1.call-start
  424.2 0.1 collective-permute-start.3
  424.2 25.3 %collective-permute-done.3 = bf16[512,1024]{1,0:T(8,128)(2,1)S(1)} collective-permute-done((bf16[512,1024]{1,0:T(8,128)(2,1)S(1)}, bf16[512,1024]{1,0:T(8,128)(2,1)S(1)}, u32[]{:S(2)}, u32[]{:S(2)}) %collective-permute-start.3) | collective-permute-done | bytes 1048608 | tf_op jit(solution)/shard_map/ppermute | solution.py:22
  449.5 24.4 %collective-permute-done.4 = bf16[512,1024]{1,0:T(8,128)(2,1)S(1)} collective-permute-done((bf16[512,1024]{1,0:T(8,128)(2,1)S(1)}, bf16[512,1024]{1,0:T(8,128)(2,1)S(1)}, u32[]{:S(2)}, u32[]{:S(2)}) %collective-permute-start.4) | collective-permute-done | bytes 1048608 | tf_op jit(solution)/shard_map/ppermute | solution.py:22
  473.9 23.6 %collective-permute-done.5 = bf16[512,1024]{1,0:T(8,128)(2,1)S(1)} collective-permute-done((bf16[512,1024]{1,0:T(8,128)(2,1)S(1)}, bf16[512,1024]{1,0:T(8,128)(2,1)S(1)}, u32[]{:S(2)}, u32[]{:S(2)}) %collective-permute-start.5) | collective-permute-done | bytes 1048608 | tf_op jit(solution)/shard_map/ppermute | solution.py:22
  497.5 8.2 %fusion.3 = bf16[512,4096]{1,0:T(8,128)(2,1)} fusion(s32[]{:T(128)S(6)} %select_n.23, bf16[512,1024]{1,0:T(8,128)(2,1)S(1)} %collective-permute-done.5, bf16[512,1024]{1,0:T(8,128)(2,1)S(1)} %collective-permute-done.4, bf16[512,1024]{1,0:T(8,128)(2,1)S(1)} %collective-permute-done.3, bf16[512,1024]{1,0:T(8,128)(2,1)S(1)} %copy-done), kind=kLoop, calls=%fused_computation.23 | loop fusion | flops 33554432 | bytes 8388612 | tf_op jit(solution)/shard_map/jit(_roll_dynamic)/concatenate | solution.py:25
  505.7 10.9 %fusion.23 = (bf16[512,1024]{1,0:T(8,128)(2,1)}, f32[512,1024]{1,0:T(8,128)}) fusion(bf16[512,4096]{1,0:T(8,128)(2,1)} %fusion.3, bf16[4096,1024]{1,0:T(8,128)(2,1)} %all-gather.15.cloned.1.call-done), kind=kOutput, calls=%fused_computation.56 | convolution fusion | flops 4295491584 | bytes 15728640 | tf_op jit(solution)/shard_map/dot_general | solution.py:38
  516.6 0.0 all-gather.11.cloned.1.call-done
  516.7 11.7 %fusion.18 = bf16[512,1024]{1,0:T(8,128)(2,1)} fusion(f32[512,1024]{1,0:T(8,128)} %get-tuple-element.8, bf16[512,1024]{1,0:T(8,128)(2,1)S(1)} %copy-done.4, bf16[512,4096]{1,0:T(8,128)(2,1)} %fusion.10, bf16[4096,1024]{1,0:T(8,128)(2,1)} %all-gather.11.cloned.1.call-done, f32[1024]{0:T(1024)S(1)} %dynamic_slice.16, ...), kind=kOutput, calls=%fused_computation.41 | convolution fusion | flops 4301783040 | bytes 16789504 | tf_op jit(solution)/shard_map/dot_general | solution.py:38
  528.4 3.8 all-to-all-start
  532.2 36.3 %all-gather.17.cloned.1.call-done = bf16[4096,1024]{1,0:T(8,128)(2,1)} async-done(((bf16[512,1024]{1,0:T(8,128)(2,1)}), bf16[4096,1024]{1,0:T(8,128)(2,1)}) %all-gather.17.cloned.1.call-update) | async-done | bytes 8388624 | tf_op jit(solution)/shard_map/all_gather | solution.py:40
  568.5 11.1 %fusion.21 = bf16[512,1024]{1,0:T(8,128)(2,1)} fusion(f32[512,1024]{1,0:T(8,128)} %get-tuple-element.10, bf16[512,1024]{1,0:T(8,128)(2,1)S(1)} %copy-done.3, bf16[512,4096]{1,0:T(8,128)(2,1)} %fusion.3, bf16[4096,1024]{1,0:T(8,128)(2,1)} %all-gather.17.cloned.1.call-done, f32[1024]{0:T(1024)S(1)} %dynamic_slice.18, f32[512]{0:T(512)S(1)} %dynamic-slice_multiply_fusion, ...), kind=kOutput, calls=%fused_computation.44 | convolution fusion | flops 4301783040 | bytes 16789504 | tf_op jit(solution)/shard_map/dot_general | solution.py:38
  579.6 4.6 all-to-all-start.1
  584.2 0.2 convert_bitcast_fusion.1
  584.4 1.5 copy.6
  585.9 24.4 %all-to-all-done.1 = bf16[4,128,1024]{2,1,0:T(8,128)(2,1)S(1)} async-done(((bf16[4,128,1024]{2,1,0:T(8,128)(2,1)}), bf16[4,128,1024]{2,1,0:T(8,128)(2,1)S(1)}, u32[]{:S(2)}, u32[]{:S(2)}) %all-to-all-start.1) | async-done | bytes 1048608 | tf_op jit(solution)/shard_map/all_to_all | solution.py:97
  610.3 0.2 convert_bitcast_fusion
  610.5 1.5 copy.7
  (25 shorter events, 0.1 us)
Async XLA Ops:
  7.2 85.9 %all-gather.13.cloned.1.call-start = ((), (), s32[]{:S(2)}) async-start(), calls=%async_computation.8 | async-start | bytes 5242880 | tf_op jit(solution)/shard_map/all_gather | solution.py:63
  7.9 166.0 %all-gather.7.cloned.1.call-start = ((), (), s32[]{:S(2)}) async-start(), calls=%async_computation.4 | async-start | bytes 5242880 | tf_op jit(solution)/shard_map/all_gather | solution.py:62
  8.6 238.9 %reduce-scatter.5.cloned.1.call-start = ((), (), s32[]{:S(2)}) async-start(), calls=%async_computation.9 | async-start | bytes 9437184 | tf_op jit(solution)/shard_map/reduce_scatter | solution.py:74
  103.6 70.3 %copy-start.2 = (bf16[512,1024]{1,0:T(8,128)(2,1)S(1)}, bf16[512,1024]{1,0:T(8,128)(2,1)}, u32[]{:S(2)}) copy-start(bf16[512,1024]{1,0:T(8,128)(2,1)} %param.4) | copy-start | bytes 3145732
  103.6 218.8 %reduce-scatter.3.cloned.1.call-start = ((), (), s32[]{:S(2)}) async-start(), calls=%async_computation.5 | async-start | bytes 9437184 | tf_op jit(solution)/shard_map/reduce_scatter | solution.py:74
  182.9 230.3 %all-gather.9.cloned.1.call-start = ((), (), s32[]{:S(2)}) async-start(), calls=%async_computation.6 | async-start | bytes 9437184 | tf_op jit(solution)/shard_map/all_gather | solution.py:40
  182.9 5.2 copy-start.1
  326.2 179.5 %all-gather.15.cloned.1.call-start = ((), (), s32[]{:S(2)}) async-start(), calls=%async_computation.10 | async-start | bytes 9437184 | tf_op jit(solution)/shard_map/all_gather | solution.py:40
  326.8 189.8 %all-gather.11.cloned.1.call-start = ((), (), s32[]{:S(2)}) async-start(), calls=%async_computation.7 | async-start | bytes 9437184 | tf_op jit(solution)/shard_map/all_gather | solution.py:40
  326.8 26.8 %collective-permute-start = (bf16[512,1024]{1,0:T(8,128)(2,1)}, bf16[512,1024]{1,0:T(8,128)(2,1)S(1)}, u32[]{:S(2)}, u32[]{:S(2)}) collective-permute-start(bf16[512,1024]{1,0:T(8,128)(2,1)} %get-tuple-element.6), channel_id=1, source_target_pairs={{0,1},{1,2},{2,3},{3,0},{4,5},{5,6},{6,7},{7,4},{8,9},{9,10},{10,1... | collective-permute-start | bytes 3145736 | tf_op jit(solution)/shard_map/ppermute | solution.py:22
  353.6 25.7 %collective-permute-start.1 = (bf16[512,1024]{1,0:T(8,128)(2,1)S(1)}, bf16[512,1024]{1,0:T(8,128)(2,1)S(1)}, u32[]{:S(2)}, u32[]{:S(2)}) collective-permute-start(bf16[512,1024]{1,0:T(8,128)(2,1)S(1)} %collective-permute-done), channel_id=1, source_target_pairs={{0,1},{1,2},{2,3},{3,0},{4,5},{5,6},{6,7},{7,4},{8,9},{9,10},{10,1... | collective-permute-start | bytes 3145736 | tf_op jit(solution)/shard_map/ppermute | solution.py:22
  379.3 24.8 %collective-permute-start.2 = (bf16[512,1024]{1,0:T(8,128)(2,1)S(1)}, bf16[512,1024]{1,0:T(8,128)(2,1)S(1)}, u32[]{:S(2)}, u32[]{:S(2)}) collective-permute-start(bf16[512,1024]{1,0:T(8,128)(2,1)S(1)} %collective-permute-done.1), channel_id=1, source_target_pairs={{0,1},{1,2},{2,3},{3,0},{4,5},{5,6},{6,7},{7,4},{8,9},{9,10},{10,1... | collective-permute-start | bytes 3145736 | tf_op jit(solution)/shard_map/ppermute | solution.py:22
  413.1 11.0 %copy-start = (bf16[512,1024]{1,0:T(8,128)(2,1)S(1)}, bf16[512,1024]{1,0:T(8,128)(2,1)}, u32[]{:S(2)}) copy-start(bf16[512,1024]{1,0:T(8,128)(2,1)} %get-tuple-element.5) | copy-start | bytes 3145732
  424.1 144.4 %all-gather.17.cloned.1.call-start = ((), (), s32[]{:S(2)}) async-start(), calls=%async_computation.11 | async-start | bytes 9437184 | tf_op jit(solution)/shard_map/all_gather | solution.py:40
  424.2 25.3 %collective-permute-start.3 = (bf16[512,1024]{1,0:T(8,128)(2,1)S(1)}, bf16[512,1024]{1,0:T(8,128)(2,1)S(1)}, u32[]{:S(2)}, u32[]{:S(2)}) collective-permute-start(bf16[512,1024]{1,0:T(8,128)(2,1)S(1)} %copy-done), channel_id=1, source_target_pairs={{0,1},{1,2},{2,3},{3,0},{4,5},{5,6},{6,7},{7,4},{8,9},{9,10},{10,1... | collective-permute-start | bytes 3145736 | tf_op jit(solution)/shard_map/ppermute | solution.py:22
  449.5 24.4 %collective-permute-start.4 = (bf16[512,1024]{1,0:T(8,128)(2,1)S(1)}, bf16[512,1024]{1,0:T(8,128)(2,1)S(1)}, u32[]{:S(2)}, u32[]{:S(2)}) collective-permute-start(bf16[512,1024]{1,0:T(8,128)(2,1)S(1)} %collective-permute-done.3), channel_id=1, source_target_pairs={{0,1},{1,2},{2,3},{3,0},{4,5},{5,6},{6,7},{7,4},{8,9},{9,10},{10,1... | collective-permute-start | bytes 3145736 | tf_op jit(solution)/shard_map/ppermute | solution.py:22
  473.9 23.6 %collective-permute-start.5 = (bf16[512,1024]{1,0:T(8,128)(2,1)S(1)}, bf16[512,1024]{1,0:T(8,128)(2,1)S(1)}, u32[]{:S(2)}, u32[]{:S(2)}) collective-permute-start(bf16[512,1024]{1,0:T(8,128)(2,1)S(1)} %collective-permute-done.4), channel_id=1, source_target_pairs={{0,1},{1,2},{2,3},{3,0},{4,5},{5,6},{6,7},{7,4},{8,9},{9,10},{10,1... | collective-permute-start | bytes 3145736 | tf_op jit(solution)/shard_map/ppermute | solution.py:22
  505.7 10.9 %copy-start.4 = (bf16[512,1024]{1,0:T(8,128)(2,1)S(1)}, bf16[512,1024]{1,0:T(8,128)(2,1)}, u32[]{:S(2)}) copy-start(bf16[512,1024]{1,0:T(8,128)(2,1)} %reduce-scatter.3.cloned.1.call-done) | copy-start | bytes 3145732
  516.6 51.8 %copy-start.3 = (bf16[512,1024]{1,0:T(8,128)(2,1)S(1)}, bf16[512,1024]{1,0:T(8,128)(2,1)}, u32[]{:S(2)}) copy-start(bf16[512,1024]{1,0:T(8,128)(2,1)} %reduce-scatter.5.cloned.1.call-done) | copy-start | bytes 3145732
  528.4 51.2 %all-to-all-start = ((bf16[4,128,1024]{2,1,0:T(8,128)(2,1)}), bf16[4,128,1024]{2,1,0:T(8,128)(2,1)S(1)}, u32[]{:S(2)}, u32[]{:S(2)}) async-start(bf16[4,128,1024]{2,1,0:T(8,128)(2,1)} %bitcast), calls=%async_computation.1 | async-start | bytes 2097152 | tf_op jit(solution)/shard_map/all_to_all | solution.py:97
  579.6 30.7 %all-to-all-start.1 = ((bf16[4,128,1024]{2,1,0:T(8,128)(2,1)}), bf16[4,128,1024]{2,1,0:T(8,128)(2,1)S(1)}, u32[]{:S(2)}, u32[]{:S(2)}) async-start(bf16[4,128,1024]{2,1,0:T(8,128)(2,1)} %bitcast.2), calls=%async_computation.3 | async-start | bytes 2097152 | tf_op jit(solution)/shard_map/all_to_all | solution.py:97
Sparse Core Ops, SparseCore 0:
  9.5 83.4 all-gather.12
  94.6 79.2 all-gather.6
  177.3 70.1 reduce-scatter.4
  250.9 71.4 reduce-scatter.2
  326.3 54.2 all-gather.8
  383.0 54.2 all-gather.14
  439.1 54.2 all-gather.10
  516.7 51.6 all-gather.16
